TPU v7x, 32 devices: a whole 2x2x4 slice. The times are simulated.
32 devices in a mesh: group: 4 (over y, core), sub: 8 (over z, x).
Axes of the slice: x: 2, y: 2, z: 4, core: 2. Of those that a mesh axis runs over, the one named last changes fastest.
Arguments:
- shared_sizes: int32 [4, 8, 2], P('group', 'sub'), may hold values from 0 to 256, as said below
- stiffness: float32 [4, 8], P('group', 'sub'), may hold values from 0.1 to 10
- load_cases: float32 [4, 8, 1024, 384], P('group', 'sub'), may hold values from -6 to 6
- schur_blocks: bfloat16 [4, 8, 1024, 1024], P('group', 'sub')
- neumann_inverse: bfloat16 [4, 8, 1024, 1024], P('group', 'sub')
- coarse_basis: bfloat16 [4, 8, 32, 1024], P('group', 'sub'), may hold values from -0.1875 to 0.1875
- coarse_dofs: int32 [4, 8, 32], P('group', 'sub'), may hold values from 0 to 511
- coarse_inverse: float32 [512, 512], P('sub'), as said below
Outputs:
- solution: float32 [4, 8, 1024, 384], P('group', 'sub')
- residual: float32 [4, 8, 1024, 384], P('group', 'sub')
Inputs may be any that keep to these rules, and one draw needn't show every extreme that they name: shared_sizes[g, s, 0] equals shared_sizes[g, s - 1, 1]; the lower share of the first and the upper share of the last subdomain of a group are 0, the other shares lie in 128 to 256, and in every group some subdomain shares exactly 256 with its upper neighbour. `coarse_inverse`: symmetric.
All inputs are finite; a program needn't handle non-finite values.
Results may differ from a plain program's by a relative error of at most 0.0075.
Values sent between devices are 32-bit elements; how exact they have to be, the bound alone decides.
No kernel may reach another device: no remote copies, remote signals or barrier semaphores. Data moves between devices by JAX's collectives and lax.ppermute only.
A program may use at most 128 MiB of HBM per device.

v0:
```python
import jax
import jax.numpy as jnp
from jax import lax
from jax.sharding import PartitionSpec as P

MAXSH = 256
ITERS = 4
OMEGA = 0.6


def from_behind(block, axis, distance):
    devices = range(lax.axis_size(axis))
    route = [(i - distance, i) for i in devices if i - distance in devices]
    return lax.ppermute(block, axis, route)


def extended(x, sides, width):
    for axis, dim in sides:
        peers, length = (lax.axis_size(axis), x.shape[dim])
        up = [(i, (i + 1) % peers) for i in range(peers - 1)]
        down = [(j, i) for i, j in up]
        last = lax.slice_in_dim(x, length - width, length, axis=dim)
        leading = lax.slice_in_dim(x, 0, width, axis=dim)
        before = lax.ppermute(last, axis, up)
        after = lax.ppermute(leading, axis, down)
        x = jnp.concatenate([before, x, after], axis=dim)
    return x


def lift_piece(tail_rows, share_size):
    slab_width = tail_rows.shape[0]
    rolled = jnp.roll(tail_rows, share_size - slab_width, axis=0)
    inside = (jnp.arange(slab_width) < share_size)[:, None]
    return jnp.where(inside, rolled, jnp.zeros_like(rolled))


def place_piece(head_rows, share_size):
    slab_width = head_rows.shape[0]
    inside = (jnp.arange(slab_width) < share_size)[:, None]
    masked = jnp.where(inside, head_rows, jnp.zeros_like(head_rows))
    return jnp.roll(masked, slab_width - share_size, axis=0)


def assemble(vector, share_up):
    unknowns = vector.shape[0]
    tail_rows = vector[unknowns - MAXSH :]
    head_rows = vector[:MAXSH]
    lifted = lift_piece(tail_rows, share_up)
    from_lower = from_behind(lifted, "sub", 1)
    from_upper = from_behind(head_rows, "sub", -1)
    placed = place_piece(from_upper, share_up)
    return jnp.concatenate(
        [head_rows + from_lower, vector[MAXSH : unknowns - MAXSH], tail_rows + placed], axis=0
    )


def on_device(
    shared_sizes,
    stiffness,
    load_cases,
    schur_blocks,
    neumann_inverse,
    coarse_basis,
    coarse_dofs,
    coarse_inverse,
):
    share_low = shared_sizes[0, 0, 0]
    share_up = shared_sizes[0, 0, 1]
    beside_all = extended(stiffness, (("sub", 1),), 1)
    own_stiff = beside_all[0, 1]
    low_weight = own_stiff / (own_stiff + beside_all[0, 0])
    up_weight = own_stiff / (own_stiff + beside_all[0, 2])
    loads = load_cases[0, 0]
    schur = schur_blocks[0, 0]
    neumann = neumann_inverse[0, 0]
    basis = coarse_basis[0, 0]
    my_dofs = coarse_dofs[0, 0]
    unknowns, cases = loads.shape
    own_count = coarse_inverse.shape[0]
    row_index = jnp.arange(unknowns)
    weight = jnp.where(
        row_index < share_low,
        low_weight,
        jnp.where(row_index >= unknowns - share_up, up_weight, jnp.float32(1.0)),
    )[:, None]
    highest = lax.Precision.HIGHEST

    def operator_residual(solution):
        return loads - jnp.dot(
            schur, solution.astype(jnp.bfloat16), preferred_element_type=jnp.float32
        )

    solution = jnp.zeros((unknowns, cases), jnp.float32)
    for sweep in range(ITERS):
        local = operator_residual(solution)
        weighted = (weight * assemble(local, share_up)).astype(jnp.bfloat16)
        coarse_terms = jnp.dot(basis, weighted, preferred_element_type=jnp.float32)
        dof_values = my_dofs.astype(jnp.float32)
        all_terms = lax.all_gather(coarse_terms, "sub", axis=0, tiled=True)
        all_dofs = lax.all_gather(dof_values, "sub", axis=0, tiled=True)
        dof_index = all_dofs.astype(jnp.int32)
        first_row = lax.axis_index("sub") * own_count
        own_select = (dof_index[:, None] == first_row + jnp.arange(own_count)[None, :]).astype(
            jnp.float32
        )
        owned = lax.dot_general(own_select, all_terms, (((0,), (0,)), ((), ())), precision=highest)
        owned = lax.psum(owned, "group")
        columns = jnp.take(coarse_inverse, dof_index, axis=1)
        partial_vals = lax.dot_general(columns, owned, (((0,), (0,)), ((), ())), precision=highest)
        partial_vals = partial_vals.reshape(-1, coarse_terms.shape[0], cases)
        received = lax.all_to_all(partial_vals, "sub", split_axis=0, concat_axis=0, tiled=True)
        picked = jnp.sum(received, axis=0)
        picked = picked.astype(jnp.bfloat16)
        correction = jnp.dot(neumann, weighted, preferred_element_type=jnp.float32)
        correction = correction + lax.dot_general(
            basis, picked, (((0,), (0,)), ((), ())), preferred_element_type=jnp.float32
        )
        solution = solution + OMEGA * assemble(weight * correction, share_up)
    residual = assemble(operator_residual(solution), share_up)
    return (solution[None, None], residual[None, None])


def solution(mesh):
    return jax.shard_map(
        on_device,
        mesh=mesh,
        in_specs=(
            P("group", "sub", None),
            P("group", "sub"),
            P("group", "sub", None, None),
            P("group", "sub", None, None),
            P("group", "sub", None, None),
            P("group", "sub", None, None),
            P("group", "sub", None),
            P("sub", None),
        ),
        out_specs=(P("group", "sub", None, None), P("group", "sub", None, None)),
        check_vma=False,
    )
```

profile of v0, /device:TPU:16, one launch (start us, length us, event | category | flops | bytes accessed | tf_op | source)
XLA Modules:
  0.0 597.5 jit_solution(9661922671992732006)
XLA Ops:
  31.0 14.9 %all-reduce = f32[256]{0:T(256)S(1)} all-reduce(f32[256]{0:T(256)S(1)} %bitcast_dynamic-update-slice_fusion), channel_id=2, replica_groups=mesh['group'=4,'sub'=8] {'sub'}, use_global_device_ids=true, to_apply=%add | all-reduce | flops 256 | bytes 2048
  63.2 27.9 %all_gather.19 = f32[256,384]{1,0:T(8,128)S(1)} all-gather(f32[32,384]{1,0:T(8,128)S(1)} %convolution_bitcast_fusion.3), channel_id=1, replica_groups=mesh['group'=4,'sub'=8] {'sub'}, dimensions={0}, use_global_device_ids=true | all-gather | bytes 442368 | tf_op jit(solution)/shard_map/all_gather | solution.py:99
  93.1 34.8 %all-reduce.6.cloned.1.call-done = f32[64,384]{1,0:T(8,128)} async-done(((f32[64,384]{1,0:T(8,128)}), f32[64,384]{1,0:T(8,128)}) %all-reduce.6.cloned.1.call-update) | async-done | bytes 98320 | tf_op jit(solution)/shard_map/psum | solution.py:107
  129.4 15.0 %all_to_all.20 = f32[8,32,384]{2,1,0:T(8,128)} all-to-all(f32[8,32,384]{2,1,0:T(8,128)S(1)} %bitcast.145), channel_id=1, replica_groups=mesh['group'=4,'sub'=8] {'sub'}, dimensions={0} | all-to-all | bytes 786432 | tf_op jit(solution)/shard_map/all_to_all | solution.py:111
  152.3 8.6 %collective-permute-done.5 = f32[256,384]{0,1:T(8,128)S(1)} collective-permute-done((f32[256,384]{0,1:T(8,128)S(1)}, f32[256,384]{0,1:T(8,128)S(1)}, u32[]{:S(2)}, u32[]{:S(2)}) %collective-permute-start.5) | collective-permute-done | bytes 393248 | tf_op jit(solution)/shard_map/ppermute | solution.py:14
  176.5 8.2 %collective-permute-done.7 = f32[256,384]{0,1:T(8,128)S(1)} collective-permute-done((f32[256,384]{0,1:T(8,128)S(1)}, f32[256,384]{0,1:T(8,128)S(1)}, u32[]{:S(2)}, u32[]{:S(2)}) %collective-permute-start.7) | collective-permute-done | bytes 393248 | tf_op jit(solution)/shard_map/ppermute | solution.py:14
  187.6 8.1 %collective-permute-done.6 = f32[256,384]{0,1:T(8,128)S(1)} collective-permute-done((f32[256,384]{0,1:T(8,128)S(1)}, f32[256,384]{0,1:T(8,128)S(1)}, u32[]{:S(2)}, u32[]{:S(2)}) %collective-permute-start.6) | collective-permute-done | bytes 393248 | tf_op jit(solution)/shard_map/ppermute | solution.py:14
  196.3 25.4 %all_gather.20 = f32[256,384]{1,0:T(8,128)S(1)} all-gather(f32[32,384]{1,0:T(8,128)S(1)} %convolution_bitcast_fusion.2), channel_id=1, replica_groups=mesh['group'=4,'sub'=8] {'sub'}, dimensions={0}, use_global_device_ids=true | all-gather | bytes 442368 | tf_op jit(solution)/shard_map/all_gather | solution.py:99
  222.8 34.4 %all-reduce.8.cloned.1.call-done = f32[64,384]{1,0:T(8,128)} async-done(((f32[64,384]{1,0:T(8,128)}), f32[64,384]{1,0:T(8,128)}) %all-reduce.8.cloned.1.call-update) | async-done | bytes 98320 | tf_op jit(solution)/shard_map/psum | solution.py:107
  258.6 14.9 %all_to_all.21 = f32[8,32,384]{2,1,0:T(8,128)} all-to-all(f32[8,32,384]{2,1,0:T(8,128)S(1)} %bitcast.146), channel_id=1, replica_groups=mesh['group'=4,'sub'=8] {'sub'}, dimensions={0} | all-to-all | bytes 786432 | tf_op jit(solution)/shard_map/all_to_all | solution.py:111
  281.7 8.6 %collective-permute-done.9 = f32[256,384]{0,1:T(8,128)S(1)} collective-permute-done((f32[256,384]{0,1:T(8,128)S(1)}, f32[256,384]{0,1:T(8,128)S(1)}, u32[]{:S(2)}, u32[]{:S(2)}) %collective-permute-start.9) | collective-permute-done | bytes 393248 | tf_op jit(solution)/shard_map/ppermute | solution.py:14
  305.9 8.2 %collective-permute-done.11 = f32[256,384]{0,1:T(8,128)S(1)} collective-permute-done((f32[256,384]{0,1:T(8,128)S(1)}, f32[256,384]{0,1:T(8,128)S(1)}, u32[]{:S(2)}, u32[]{:S(2)}) %collective-permute-start.11) | collective-permute-done | bytes 393248 | tf_op jit(solution)/shard_map/ppermute | solution.py:14
  325.7 25.4 %all_gather.21 = f32[256,384]{1,0:T(8,128)S(1)} all-gather(f32[32,384]{1,0:T(8,128)S(1)} %convolution_bitcast_fusion.1), channel_id=1, replica_groups=mesh['group'=4,'sub'=8] {'sub'}, dimensions={0}, use_global_device_ids=true | all-gather | bytes 442368 | tf_op jit(solution)/shard_map/all_gather | solution.py:99
  352.2 34.4 %all-reduce.10.cloned.1.call-done = f32[64,384]{1,0:T(8,128)} async-done(((f32[64,384]{1,0:T(8,128)}), f32[64,384]{1,0:T(8,128)}) %all-reduce.10.cloned.1.call-update) | async-done | bytes 98320 | tf_op jit(solution)/shard_map/psum | solution.py:107
  388.0 14.9 %all_to_all.22 = f32[8,32,384]{2,1,0:T(8,128)} all-to-all(f32[8,32,384]{2,1,0:T(8,128)S(1)} %bitcast.147), channel_id=1, replica_groups=mesh['group'=4,'sub'=8] {'sub'}, dimensions={0} | all-to-all | bytes 786432 | tf_op jit(solution)/shard_map/all_to_all | solution.py:111
  411.1 8.6 %collective-permute-done.13 = f32[256,384]{0,1:T(8,128)S(1)} collective-permute-done((f32[256,384]{0,1:T(8,128)S(1)}, f32[256,384]{0,1:T(8,128)S(1)}, u32[]{:S(2)}, u32[]{:S(2)}) %collective-permute-start.13) | collective-permute-done | bytes 393248 | tf_op jit(solution)/shard_map/ppermute | solution.py:14
  435.4 8.2 %collective-permute-done.15 = f32[256,384]{0,1:T(8,128)S(1)} collective-permute-done((f32[256,384]{0,1:T(8,128)S(1)}, f32[256,384]{0,1:T(8,128)S(1)}, u32[]{:S(2)}, u32[]{:S(2)}) %collective-permute-start.15) | collective-permute-done | bytes 393248 | tf_op jit(solution)/shard_map/ppermute | solution.py:14
  446.5 8.1 %collective-permute-done.14 = f32[256,384]{0,1:T(8,128)S(1)} collective-permute-done((f32[256,384]{0,1:T(8,128)S(1)}, f32[256,384]{0,1:T(8,128)S(1)}, u32[]{:S(2)}, u32[]{:S(2)}) %collective-permute-start.14) | collective-permute-done | bytes 393248 | tf_op jit(solution)/shard_map/ppermute | solution.py:14
  455.2 25.4 %all_gather.22 = f32[256,384]{1,0:T(8,128)S(1)} all-gather(f32[32,384]{1,0:T(8,128)S(1)} %convolution_bitcast_fusion), channel_id=1, replica_groups=mesh['group'=4,'sub'=8] {'sub'}, dimensions={0}, use_global_device_ids=true | all-gather | bytes 442368 | tf_op jit(solution)/shard_map/all_gather | solution.py:99
  481.6 34.4 %all-reduce.12.cloned.1.call-done = f32[64,384]{1,0:T(8,128)} async-done(((f32[64,384]{1,0:T(8,128)}), f32[64,384]{1,0:T(8,128)}) %all-reduce.12.cloned.1.call-update) | async-done | bytes 98320 | tf_op jit(solution)/shard_map/psum | solution.py:107
  517.5 14.9 %all_to_all.23 = f32[8,32,384]{2,1,0:T(8,128)} all-to-all(f32[8,32,384]{2,1,0:T(8,128)S(1)} %bitcast.144), channel_id=1, replica_groups=mesh['group'=4,'sub'=8] {'sub'}, dimensions={0} | all-to-all | bytes 786432 | tf_op jit(solution)/shard_map/all_to_all | solution.py:111
  540.6 8.6 %collective-permute-done.17 = f32[256,384]{0,1:T(8,128)S(1)} collective-permute-done((f32[256,384]{0,1:T(8,128)S(1)}, f32[256,384]{0,1:T(8,128)S(1)}, u32[]{:S(2)}, u32[]{:S(2)}) %collective-permute-start.17) | collective-permute-done | bytes 393248 | tf_op jit(solution)/shard_map/ppermute | solution.py:14
  552.6 8.7 %collective-permute-done.16 = f32[256,384]{0,1:T(8,128)S(1)} collective-permute-done((f32[256,384]{0,1:T(8,128)S(1)}, f32[256,384]{0,1:T(8,128)S(1)}, u32[]{:S(2)}, u32[]{:S(2)}) %collective-permute-start.16) | collective-permute-done | bytes 393248 | tf_op jit(solution)/shard_map/ppermute | solution.py:14
  565.0 8.2 %collective-permute-done.19 = f32[256,384]{0,1:T(8,128)S(1)} collective-permute-done((f32[256,384]{0,1:T(8,128)S(1)}, f32[256,384]{0,1:T(8,128)S(1)}, u32[]{:S(2)}, u32[]{:S(2)}) %collective-permute-start.19) | collective-permute-done | bytes 393248 | tf_op jit(solution)/shard_map/ppermute | solution.py:14
  (223 shorter events, 168.8 us)
Async XLA Ops:
  7.2 120.8 %all-reduce.6.cloned.1.call-start = ((), (), s32[]{:S(2)}) async-start(), calls=%async_computation.4 | async-start | bytes 196608 | tf_op jit(solution)/shard_map/psum | solution.py:107
  7.2 45.2 %collective-permute-start.1 = (f32[1,1]{1,0:T(1,128)}, f32[1,1]{1,0:T(1,128)}, u32[]{:S(2)}, u32[]{:S(2)}) collective-permute-start(f32[1,1]{1,0:T(1,128)} %param.13), channel_id=1, source_target_pairs={{1,0},{2,1},{3,2},{4,3},{5,4},{6,5},{7,6},{9,8},{10,9},{11,10},{12... | collective-permute-start | bytes 20 | tf_op jit(solution)/shard_map/ppermute | solution.py:25
  10.7 42.5 %collective-permute-start = (f32[1,1]{1,0:T(1,128)}, f32[1,1]{1,0:T(1,128)}, u32[]{:S(2)}, u32[]{:S(2)}) collective-permute-start(f32[1,1]{1,0:T(1,128)} %param.13), channel_id=1, source_target_pairs={{0,1},{1,2},{2,3},{3,4},{4,5},{5,6},{6,7},{8,9},{9,10},{10,11},{11... | collective-permute-start | bytes 20 | tf_op jit(solution)/shard_map/ppermute | solution.py:24
  20.8 25.8 %collective-permute-start.3 = (f32[256,384]{0,1:T(8,128)}, f32[256,384]{0,1:T(8,128)S(1)}, u32[]{:S(2)}, u32[]{:S(2)}) collective-permute-start(f32[256,384]{0,1:T(8,128)} %get-tuple-element.51), channel_id=1, source_target_pairs={{1,0},{2,1},{3,2},{4,3},{5,4},{6,5},{7,6},{9,8},{10,9},{11,10},{12... | collective-permute-start | bytes 1179656 | tf_op jit(solution)/shard_map/ppermute | solution.py:14
  49.6 11.0 %collective-permute-start.2 = (f32[256,384]{0,1:T(8,128)}, f32[256,384]{0,1:T(8,128)}, u32[]{:S(2)}, u32[]{:S(2)}) collective-permute-start(f32[256,384]{0,1:T(8,128)} %get-tuple-element.70), channel_id=1, source_target_pairs={{0,1},{1,2},{2,3},{3,4},{4,5},{5,6},{6,7},{8,9},{9,10},{10,11},{11... | collective-permute-start | bytes 1179656 | tf_op jit(solution)/shard_map/ppermute | solution.py:14
  92.2 165.0 %all-reduce.8.cloned.1.call-start = ((), (), s32[]{:S(2)}) async-start(), calls=%async_computation.5 | async-start | bytes 196608 | tf_op jit(solution)/shard_map/psum | solution.py:107
  149.1 11.8 %collective-permute-start.5 = (f32[256,384]{0,1:T(8,128)S(1)}, f32[256,384]{0,1:T(8,128)S(1)}, u32[]{:S(2)}, u32[]{:S(2)}) collective-permute-start(f32[256,384]{0,1:T(8,128)S(1)} %get-tuple-element.47), channel_id=1, source_target_pairs={{1,0},{2,1},{3,2},{4,3},{5,4},{6,5},{7,6},{9,8},{10,9},{11,10},{12... | collective-permute-start | bytes 1179656 | tf_op jit(solution)/shard_map/ppermute | solution.py:14
  161.2 11.9 %collective-permute-start.4 = (f32[256,384]{0,1:T(8,128)S(1)}, f32[256,384]{0,1:T(8,128)S(1)}, u32[]{:S(2)}, u32[]{:S(2)}) collective-permute-start(f32[256,384]{0,1:T(8,128)S(1)} %get-tuple-element.66), channel_id=1, source_target_pairs={{0,1},{1,2},{2,3},{3,4},{4,5},{5,6},{6,7},{8,9},{9,10},{10,11},{11... | collective-permute-start | bytes 1179656 | tf_op jit(solution)/shard_map/ppermute | solution.py:14
  174.6 10.1 %collective-permute-start.7 = (f32[256,384]{0,1:T(8,128)S(1)}, f32[256,384]{0,1:T(8,128)S(1)}, u32[]{:S(2)}, u32[]{:S(2)}) collective-permute-start(f32[256,384]{0,1:T(8,128)S(1)} %get-tuple-element.41), channel_id=1, source_target_pairs={{1,0},{2,1},{3,2},{4,3},{5,4},{6,5},{7,6},{9,8},{10,9},{11,10},{12... | collective-permute-start | bytes 1179656 | tf_op jit(solution)/shard_map/ppermute | solution.py:14
  185.0 10.7 %collective-permute-start.6 = (f32[256,384]{0,1:T(8,128)S(1)}, f32[256,384]{0,1:T(8,128)S(1)}, u32[]{:S(2)}, u32[]{:S(2)}) collective-permute-start(f32[256,384]{0,1:T(8,128)S(1)} %get-tuple-element.64), channel_id=1, source_target_pairs={{0,1},{1,2},{2,3},{3,4},{4,5},{5,6},{6,7},{8,9},{9,10},{10,11},{11... | collective-permute-start | bytes 1179656 | tf_op jit(solution)/shard_map/ppermute | solution.py:14
  222.7 163.8 %all-reduce.10.cloned.1.call-start = ((), (), s32[]{:S(2)}) async-start(), calls=%async_computation.6 | async-start | bytes 196608 | tf_op jit(solution)/shard_map/psum | solution.py:107
  278.5 11.8 %collective-permute-start.9 = (f32[256,384]{0,1:T(8,128)S(1)}, f32[256,384]{0,1:T(8,128)S(1)}, u32[]{:S(2)}, u32[]{:S(2)}) collective-permute-start(f32[256,384]{0,1:T(8,128)S(1)} %get-tuple-element.37), channel_id=1, source_target_pairs={{1,0},{2,1},{3,2},{4,3},{5,4},{6,5},{7,6},{9,8},{10,9},{11,10},{12... | collective-permute-start | bytes 1179656 | tf_op jit(solution)/shard_map/ppermute | solution.py:14
  290.6 11.9 %collective-permute-start.8 = (f32[256,384]{0,1:T(8,128)S(1)}, f32[256,384]{0,1:T(8,128)S(1)}, u32[]{:S(2)}, u32[]{:S(2)}) collective-permute-start(f32[256,384]{0,1:T(8,128)S(1)} %get-tuple-element.62), channel_id=1, source_target_pairs={{0,1},{1,2},{2,3},{3,4},{4,5},{5,6},{6,7},{8,9},{9,10},{10,11},{11... | collective-permute-start | bytes 1179656 | tf_op jit(solution)/shard_map/ppermute | solution.py:14
  303.9 10.1 %collective-permute-start.11 = (f32[256,384]{0,1:T(8,128)S(1)}, f32[256,384]{0,1:T(8,128)S(1)}, u32[]{:S(2)}, u32[]{:S(2)}) collective-permute-start(f32[256,384]{0,1:T(8,128)S(1)} %get-tuple-element.31), channel_id=1, source_target_pairs={{1,0},{2,1},{3,2},{4,3},{5,4},{6,5},{7,6},{9,8},{10,9},{11,10},{12... | collective-permute-start | bytes 1179656 | tf_op jit(solution)/shard_map/ppermute | solution.py:14
  314.3 10.7 %collective-permute-start.10 = (f32[256,384]{0,1:T(8,128)S(1)}, f32[256,384]{0,1:T(8,128)S(1)}, u32[]{:S(2)}, u32[]{:S(2)}) collective-permute-start(f32[256,384]{0,1:T(8,128)S(1)} %get-tuple-element.60), channel_id=1, source_target_pairs={{0,1},{1,2},{2,3},{3,4},{4,5},{5,6},{6,7},{8,9},{9,10},{10,11},{11... | collective-permute-start | bytes 1179656 | tf_op jit(solution)/shard_map/ppermute | solution.py:14
  352.1 163.9 %all-reduce.12.cloned.1.call-start = ((), (), s32[]{:S(2)}) async-start(), calls=%async_computation.7 | async-start | bytes 196608 | tf_op jit(solution)/shard_map/psum | solution.py:107
  407.9 11.9 %collective-permute-start.13 = (f32[256,384]{0,1:T(8,128)S(1)}, f32[256,384]{0,1:T(8,128)S(1)}, u32[]{:S(2)}, u32[]{:S(2)}) collective-permute-start(f32[256,384]{0,1:T(8,128)S(1)} %get-tuple-element.27), channel_id=1, source_target_pairs={{1,0},{2,1},{3,2},{4,3},{5,4},{6,5},{7,6},{9,8},{10,9},{11,10},{12... | collective-permute-start | bytes 1179656 | tf_op jit(solution)/shard_map/ppermute | solution.py:14
  420.0 11.9 %collective-permute-start.12 = (f32[256,384]{0,1:T(8,128)S(1)}, f32[256,384]{0,1:T(8,128)S(1)}, u32[]{:S(2)}, u32[]{:S(2)}) collective-permute-start(f32[256,384]{0,1:T(8,128)S(1)} %get-tuple-element.58), channel_id=1, source_target_pairs={{0,1},{1,2},{2,3},{3,4},{4,5},{5,6},{6,7},{8,9},{9,10},{10,11},{11... | collective-permute-start | bytes 1179656 | tf_op jit(solution)/shard_map/ppermute | solution.py:14
  433.4 10.1 %collective-permute-start.15 = (f32[256,384]{0,1:T(8,128)S(1)}, f32[256,384]{0,1:T(8,128)S(1)}, u32[]{:S(2)}, u32[]{:S(2)}) collective-permute-start(f32[256,384]{0,1:T(8,128)S(1)} %get-tuple-element.21), channel_id=1, source_target_pairs={{1,0},{2,1},{3,2},{4,3},{5,4},{6,5},{7,6},{9,8},{10,9},{11,10},{12... | collective-permute-start | bytes 1179656 | tf_op jit(solution)/shard_map/ppermute | solution.py:14
  443.9 10.7 %collective-permute-start.14 = (f32[256,384]{0,1:T(8,128)S(1)}, f32[256,384]{0,1:T(8,128)S(1)}, u32[]{:S(2)}, u32[]{:S(2)}) collective-permute-start(f32[256,384]{0,1:T(8,128)S(1)} %get-tuple-element.56), channel_id=1, source_target_pairs={{0,1},{1,2},{2,3},{3,4},{4,5},{5,6},{6,7},{8,9},{9,10},{10,11},{11... | collective-permute-start | bytes 1179656 | tf_op jit(solution)/shard_map/ppermute | solution.py:14
  537.3 11.8 %collective-permute-start.17 = (f32[256,384]{0,1:T(8,128)S(1)}, f32[256,384]{0,1:T(8,128)S(1)}, u32[]{:S(2)}, u32[]{:S(2)}) collective-permute-start(f32[256,384]{0,1:T(8,128)S(1)} %get-tuple-element.17), channel_id=1, source_target_pairs={{1,0},{2,1},{3,2},{4,3},{5,4},{6,5},{7,6},{9,8},{10,9},{11,10},{12... | collective-permute-start | bytes 1179656 | tf_op jit(solution)/shard_map/ppermute | solution.py:14
  549.5 11.9 %collective-permute-start.16 = (f32[256,384]{0,1:T(8,128)S(1)}, f32[256,384]{0,1:T(8,128)S(1)}, u32[]{:S(2)}, u32[]{:S(2)}) collective-permute-start(f32[256,384]{0,1:T(8,128)S(1)} %get-tuple-element.54), channel_id=1, source_target_pairs={{0,1},{1,2},{2,3},{3,4},{4,5},{5,6},{6,7},{8,9},{9,10},{10,11},{11... | collective-permute-start | bytes 1179656 | tf_op jit(solution)/shard_map/ppermute | solution.py:14
  563.1 10.1 %collective-permute-start.19 = (f32[256,384]{0,1:T(8,128)S(1)}, f32[256,384]{0,1:T(8,128)S(1)}, u32[]{:S(2)}, u32[]{:S(2)}) collective-permute-start(f32[256,384]{0,1:T(8,128)S(1)} %get-tuple-element.11), channel_id=1, source_target_pairs={{1,0},{2,1},{3,2},{4,3},{5,4},{6,5},{7,6},{9,8},{10,9},{11,10},{12... | collective-permute-start | bytes 1179656 | tf_op jit(solution)/shard_map/ppermute | solution.py:14
  574.3 10.9 %collective-permute-start.18 = (f32[256,384]{0,1:T(8,128)}, f32[256,384]{0,1:T(8,128)}, u32[]{:S(2)}, u32[]{:S(2)}) collective-permute-start(f32[256,384]{0,1:T(8,128)} %get-tuple-element.52), channel_id=1, source_target_pairs={{0,1},{1,2},{2,3},{3,4},{4,5},{5,6},{6,7},{8,9},{9,10},{10,11},{11... | collective-permute-start | bytes 1179656 | tf_op jit(solution)/shard_map/ppermute | solution.py:14
  (52 other events, 408.4 us)
Sparse Core Ops, SparseCore 0:
  92.3 35.5 all-reduce.5
  222.9 34.2 all-reduce.7
  352.2 34.2 all-reduce.9
  481.7 34.2 all-reduce.11
where the time goes:
time: 599 us; the launch traced here: 598 us
  waiting for transfers between devices  271 us (45%)
  blocking collectives  179 us (30%)
  starting transfers between devices  55.8 us (9%)
  matrix products  30 us (5%)
  local copies, waits for them, and re-layouts  23.2 us (4%)
  between operations  19.8 us (3%)
  other arithmetic  18.8 us (3%)
    psum x4, waiting for transfers between devices, on_device(): owned = lax.psum(owned, 'group')  138 us
    ppermute x18, waiting for transfers between devices, from_behind(): return lax.ppermute(block, axis, route)  133 us
    all_gather x4, blocking collectives, on_device(): all_terms = lax.all_gather(coarse_terms, 'sub', axis=0, tiled=True)  104 us
    all_to_all x4, blocking collectives, on_device(): lax.all_to_all(partial_vals, 'sub', split_axis=0, concat_axis=0, tiled=True)  59.6 us
    ppermute x18, starting transfers between devices, from_behind(): return lax.ppermute(block, axis, route)  49.6 us
    unnamed x108, local copies, waits for them, and re-layouts  15.7 us
    unnamed x1, blocking collectives  14.9 us
  transfers between devices with their start and end apart: 24, of which 21 were waited for; matrix products, arithmetic and copies ran while one was open for 4% of the time, Pallas kernels for 0%

commit v1 on v0

--- a/solution.py
+++ b/solution.py
@@ -6,6 +6,17 @@
 MAXSH = 256
 ITERS = 4
 OMEGA = 0.6
+
+
+def gather_by_hops(block, axis, along):
+    n_dev = lax.axis_size(axis)
+    right = [(i, (i + 1) % n_dev) for i in range(n_dev)]
+    blocks = [block]
+    for stride in range(1, n_dev):
+        blocks = [lax.ppermute(blocks[0], axis, right), *blocks]
+    full = jnp.concatenate(blocks, axis=along)
+    turn = (lax.axis_index(axis) + 1) * blocks[-1].shape[along]
+    return jnp.roll(full, turn, axis=along)
 
 
 def from_behind(block, axis, distance):
@@ -96,7 +107,7 @@
         weighted = (weight * assemble(local, share_up)).astype(jnp.bfloat16)
         coarse_terms = jnp.dot(basis, weighted, preferred_element_type=jnp.float32)
         dof_values = my_dofs.astype(jnp.float32)
-        all_terms = lax.all_gather(coarse_terms, "sub", axis=0, tiled=True)
+        all_terms = gather_by_hops(coarse_terms, "sub", 0)
         all_dofs = lax.all_gather(dof_values, "sub", axis=0, tiled=True)
         dof_index = all_dofs.astype(jnp.int32)
         first_row = lax.axis_index("sub") * own_count

time: 599 us -> 656 us (1.095)
  waiting for transfers between devices: 271 us -> 422 us
  blocking collectives: 179 us -> 82.1 us
    ppermute x0 -> x28, waiting for transfers between devices: none -> 131 us  [gather_by_hops(): blocks = [lax.ppermute(blocks[0], axis, right), *blocks]]
    all_gather x4 -> x0, blocking collectives: 104 us -> none  [on_device(): all_terms = lax.all_gather(coarse_terms, 'sub', axis=0, tiled=True)]
    psum x4, waiting for transfers between devices: 138 us -> 155 us  [on_device(): owned = lax.psum(owned, 'group')]
    unnamed x1, blocking collectives: 14.9 us -> 22.5 us
    unnamed x108 -> x134, local copies, waits for them, and re-layouts: 15.7 us -> 15.2 us
  transfers between devices with their start and end apart: 24 -> 52, of which waited for: 21 -> 48; matrix products, arithmetic and copies ran while one was open for 4% -> 2% of each run, Pallas kernels for 0% -> 0%
where the time goes in v1:
time: 656 us; the launch traced here: 654 us
  waiting for transfers between devices  422 us (64%)
  blocking collectives  82.1 us (13%)
  starting transfers between devices  60.9 us (9%)
  matrix products  30.1 us (5%)
  local copies, waits for them, and re-layouts  21.8 us (3%)
  between operations  20 us (3%)
  other arithmetic  17.6 us (3%)
    psum x4, waiting for transfers between devices, on_device(): owned = lax.psum(owned, 'group')  155 us
    ppermute x18, waiting for transfers between devices, from_behind(): return lax.ppermute(block, axis, route)  136 us
    ppermute x28, waiting for transfers between devices, gather_by_hops(): blocks = [lax.ppermute(blocks[0], axis, right), *blocks]  131 us
    all_to_all x4, blocking collectives, on_device(): lax.all_to_all(partial_vals, 'sub', split_axis=0, concat_axis=0, tiled=True)  59.6 us
    ppermute x18, starting transfers between devices, from_behind(): return lax.ppermute(block, axis, route)  50.1 us
    unnamed x1, blocking collectives  22.5 us
    unnamed x134, local copies, waits for them, and re-layouts  15.2 us
  transfers between devices with their start and end apart: 52, of which 48 were waited for; matrix products, arithmetic and copies ran while one was open for 2% of the time, Pallas kernels for 0%

profile of v1, /device:TPU:16, one launch (start us, length us, event | category | flops | bytes accessed | tf_op | source)
XLA Modules:
  0.0 654.4 jit_solution(1018249831611161389)
XLA Ops:
  61.5 22.5 %all-reduce = f32[256]{0:T(256)S(1)} all-reduce(f32[256]{0:T(256)S(1)} %bitcast_dynamic-update-slice_fusion), channel_id=2, replica_groups=mesh['group'=4,'sub'=8] {'sub'}, use_global_device_ids=true, to_apply=%add | all-reduce | flops 256 | bytes 2048
  101.1 39.0 %all-reduce.6.cloned.1.call-done = f32[64,384]{1,0:T(8,128)} async-done(((f32[64,384]{1,0:T(8,128)}), f32[64,384]{1,0:T(8,128)}) %all-reduce.6.cloned.1.call-update) | async-done | bytes 98320 | tf_op jit(solution)/shard_map/psum | solution.py:118
  141.5 15.0 %all_to_all.20 = f32[8,32,384]{2,1,0:T(8,128)} all-to-all(f32[8,32,384]{2,1,0:T(8,128)S(1)} %bitcast.141), channel_id=1, replica_groups=mesh['group'=4,'sub'=8] {'sub'}, dimensions={0} | all-to-all | bytes 786432 | tf_op jit(solution)/shard_map/all_to_all | solution.py:122
  164.5 8.6 %collective-permute-done.12 = f32[256,384]{0,1:T(8,128)S(1)} collective-permute-done((f32[256,384]{0,1:T(8,128)S(1)}, f32[256,384]{0,1:T(8,128)S(1)}, u32[]{:S(2)}, u32[]{:S(2)}) %collective-permute-start.12) | collective-permute-done | bytes 393248 | tf_op jit(solution)/shard_map/ppermute | solution.py:25
  177.4 7.9 %collective-permute-done.11 = f32[256,384]{0,1:T(8,128)S(1)} collective-permute-done((f32[256,384]{0,1:T(8,128)S(1)}, f32[256,384]{0,1:T(8,128)S(1)}, u32[]{:S(2)}, u32[]{:S(2)}) %collective-permute-start.11) | collective-permute-done | bytes 393248 | tf_op jit(solution)/shard_map/ppermute | solution.py:25
  188.6 8.2 %collective-permute-done.14 = f32[256,384]{0,1:T(8,128)S(1)} collective-permute-done((f32[256,384]{0,1:T(8,128)S(1)}, f32[256,384]{0,1:T(8,128)S(1)}, u32[]{:S(2)}, u32[]{:S(2)}) %collective-permute-start.14) | collective-permute-done | bytes 393248 | tf_op jit(solution)/shard_map/ppermute | solution.py:25
  199.8 8.4 %collective-permute-done.13 = f32[256,384]{0,1:T(8,128)S(1)} collective-permute-done((f32[256,384]{0,1:T(8,128)S(1)}, f32[256,384]{0,1:T(8,128)S(1)}, u32[]{:S(2)}, u32[]{:S(2)}) %collective-permute-start.13) | collective-permute-done | bytes 393248 | tf_op jit(solution)/shard_map/ppermute | solution.py:25
  245.5 38.8 %all-reduce.8.cloned.1.call-done = f32[64,384]{1,0:T(8,128)} async-done(((f32[64,384]{1,0:T(8,128)}), f32[64,384]{1,0:T(8,128)}) %all-reduce.8.cloned.1.call-update) | async-done | bytes 98320 | tf_op jit(solution)/shard_map/psum | solution.py:118
  285.7 14.9 %all_to_all.21 = f32[8,32,384]{2,1,0:T(8,128)} all-to-all(f32[8,32,384]{2,1,0:T(8,128)S(1)} %bitcast.142), channel_id=1, replica_groups=mesh['group'=4,'sub'=8] {'sub'}, dimensions={0} | all-to-all | bytes 786432 | tf_op jit(solution)/shard_map/all_to_all | solution.py:122
  308.7 8.6 %collective-permute-done.23 = f32[256,384]{0,1:T(8,128)S(1)} collective-permute-done((f32[256,384]{0,1:T(8,128)S(1)}, f32[256,384]{0,1:T(8,128)S(1)}, u32[]{:S(2)}, u32[]{:S(2)}) %collective-permute-start.23) | collective-permute-done | bytes 393248 | tf_op jit(solution)/shard_map/ppermute | solution.py:25
  321.8 7.8 %collective-permute-done.22 = f32[256,384]{0,1:T(8,128)S(1)} collective-permute-done((f32[256,384]{0,1:T(8,128)S(1)}, f32[256,384]{0,1:T(8,128)S(1)}, u32[]{:S(2)}, u32[]{:S(2)}) %collective-permute-start.22) | collective-permute-done | bytes 393248 | tf_op jit(solution)/shard_map/ppermute | solution.py:25
  333.0 8.2 %collective-permute-done.25 = f32[256,384]{0,1:T(8,128)S(1)} collective-permute-done((f32[256,384]{0,1:T(8,128)S(1)}, f32[256,384]{0,1:T(8,128)S(1)}, u32[]{:S(2)}, u32[]{:S(2)}) %collective-permute-start.25) | collective-permute-done | bytes 393248 | tf_op jit(solution)/shard_map/ppermute | solution.py:25
  344.1 8.5 %collective-permute-done.24 = f32[256,384]{0,1:T(8,128)S(1)} collective-permute-done((f32[256,384]{0,1:T(8,128)S(1)}, f32[256,384]{0,1:T(8,128)S(1)}, u32[]{:S(2)}, u32[]{:S(2)}) %collective-permute-start.24) | collective-permute-done | bytes 393248 | tf_op jit(solution)/shard_map/ppermute | solution.py:25
  389.9 38.7 %all-reduce.10.cloned.1.call-done = f32[64,384]{1,0:T(8,128)} async-done(((f32[64,384]{1,0:T(8,128)}), f32[64,384]{1,0:T(8,128)}) %all-reduce.10.cloned.1.call-update) | async-done | bytes 98320 | tf_op jit(solution)/shard_map/psum | solution.py:118
  430.0 14.9 %all_to_all.22 = f32[8,32,384]{2,1,0:T(8,128)} all-to-all(f32[8,32,384]{2,1,0:T(8,128)S(1)} %bitcast.143), channel_id=1, replica_groups=mesh['group'=4,'sub'=8] {'sub'}, dimensions={0} | all-to-all | bytes 786432 | tf_op jit(solution)/shard_map/all_to_all | solution.py:122
  453.1 8.6 %collective-permute-done.34 = f32[256,384]{0,1:T(8,128)S(1)} collective-permute-done((f32[256,384]{0,1:T(8,128)S(1)}, f32[256,384]{0,1:T(8,128)S(1)}, u32[]{:S(2)}, u32[]{:S(2)}) %collective-permute-start.34) | collective-permute-done | bytes 393248 | tf_op jit(solution)/shard_map/ppermute | solution.py:25
  466.0 7.9 %collective-permute-done.33 = f32[256,384]{0,1:T(8,128)S(1)} collective-permute-done((f32[256,384]{0,1:T(8,128)S(1)}, f32[256,384]{0,1:T(8,128)S(1)}, u32[]{:S(2)}, u32[]{:S(2)}) %collective-permute-start.33) | collective-permute-done | bytes 393248 | tf_op jit(solution)/shard_map/ppermute | solution.py:25
  477.4 8.2 %collective-permute-done.36 = f32[256,384]{0,1:T(8,128)S(1)} collective-permute-done((f32[256,384]{0,1:T(8,128)S(1)}, f32[256,384]{0,1:T(8,128)S(1)}, u32[]{:S(2)}, u32[]{:S(2)}) %collective-permute-start.36) | collective-permute-done | bytes 393248 | tf_op jit(solution)/shard_map/ppermute | solution.py:25
  488.5 8.5 %collective-permute-done.35 = f32[256,384]{0,1:T(8,128)S(1)} collective-permute-done((f32[256,384]{0,1:T(8,128)S(1)}, f32[256,384]{0,1:T(8,128)S(1)}, u32[]{:S(2)}, u32[]{:S(2)}) %collective-permute-start.35) | collective-permute-done | bytes 393248 | tf_op jit(solution)/shard_map/ppermute | solution.py:25
  534.3 38.7 %all-reduce.12.cloned.1.call-done = f32[64,384]{1,0:T(8,128)} async-done(((f32[64,384]{1,0:T(8,128)}), f32[64,384]{1,0:T(8,128)}) %all-reduce.12.cloned.1.call-update) | async-done | bytes 98320 | tf_op jit(solution)/shard_map/psum | solution.py:118
  574.4 14.9 %all_to_all.23 = f32[8,32,384]{2,1,0:T(8,128)} all-to-all(f32[8,32,384]{2,1,0:T(8,128)S(1)} %bitcast.140), channel_id=1, replica_groups=mesh['group'=4,'sub'=8] {'sub'}, dimensions={0} | all-to-all | bytes 786432 | tf_op jit(solution)/shard_map/all_to_all | solution.py:122
  597.5 8.6 %collective-permute-done.45 = f32[256,384]{0,1:T(8,128)S(1)} collective-permute-done((f32[256,384]{0,1:T(8,128)S(1)}, f32[256,384]{0,1:T(8,128)S(1)}, u32[]{:S(2)}, u32[]{:S(2)}) %collective-permute-start.45) | collective-permute-done | bytes 393248 | tf_op jit(solution)/shard_map/ppermute | solution.py:25
  609.6 8.7 %collective-permute-done.44 = f32[256,384]{0,1:T(8,128)S(1)} collective-permute-done((f32[256,384]{0,1:T(8,128)S(1)}, f32[256,384]{0,1:T(8,128)S(1)}, u32[]{:S(2)}, u32[]{:S(2)}) %collective-permute-start.44) | collective-permute-done | bytes 393248 | tf_op jit(solution)/shard_map/ppermute | solution.py:25
  622.0 8.2 %collective-permute-done.47 = f32[256,384]{0,1:T(8,128)S(1)} collective-permute-done((f32[256,384]{0,1:T(8,128)S(1)}, f32[256,384]{0,1:T(8,128)S(1)}, u32[]{:S(2)}, u32[]{:S(2)}) %collective-permute-start.47) | collective-permute-done | bytes 393248 | tf_op jit(solution)/shard_map/ppermute | solution.py:25
  (305 shorter events, 272.1 us)
Async XLA Ops:
  7.2 132.9 %all-reduce.6.cloned.1.call-start = ((), (), s32[]{:S(2)}) async-start(), calls=%async_computation.4 | async-start | bytes 196608 | tf_op jit(solution)/shard_map/psum | solution.py:118
  14.0 12.7 %collective-permute-start.3 = (f32[256,384]{0,1:T(8,128)S(1)}, f32[256,384]{0,1:T(8,128)S(1)}, u32[]{:S(2)}, u32[]{:S(2)}) collective-permute-start(f32[256,384]{0,1:T(8,128)S(1)} %get-tuple-element.49), channel_id=1, source_target_pairs={{1,0},{2,1},{3,2},{4,3},{5,4},{6,5},{7,6},{9,8},{10,9},{11,10},{12... | collective-permute-start | bytes 1179656 | tf_op jit(solution)/shard_map/ppermute | solution.py:25
  27.8 15.5 %collective-permute-start.2 = (f32[256,384]{0,1:T(8,128)}, f32[256,384]{0,1:T(8,128)}, u32[]{:S(2)}, u32[]{:S(2)}) collective-permute-start(f32[256,384]{0,1:T(8,128)} %get-tuple-element.68), channel_id=1, source_target_pairs={{0,1},{1,2},{2,3},{3,4},{4,5},{5,6},{6,7},{8,9},{9,10},{10,11},{11... | collective-permute-start | bytes 1179656 | tf_op jit(solution)/shard_map/ppermute | solution.py:25
  32.1 9.2 %collective-permute-start.1 = (f32[1,1]{1,0:T(1,128)}, f32[1,1]{1,0:T(1,128)}, u32[]{:S(2)}, u32[]{:S(2)}) collective-permute-start(f32[1,1]{1,0:T(1,128)} %param.13), channel_id=1, source_target_pairs={{1,0},{2,1},{3,2},{4,3},{5,4},{6,5},{7,6},{9,8},{10,9},{11,10},{12... | collective-permute-start | bytes 20 | tf_op jit(solution)/shard_map/ppermute | solution.py:36
  61.4 22.6 %collective-permute-start.7 = (f32[32,384]{1,0:T(8,128)S(1)}, f32[32,384]{1,0:T(8,128)S(1)}, u32[]{:S(2)}, u32[]{:S(2)}) collective-permute-start(f32[32,384]{1,0:T(8,128)S(1)} %collective-permute-done.6), channel_id=1, source_target_pairs={{0,1},{1,2},{2,3},{3,4},{4,5},{5,6},{6,7},{7,0},{8,9},{9,10},{10,1... | collective-permute-start | bytes 147464 | tf_op jit(solution)/shard_map/ppermute | solution.py:16
  100.2 184.1 %all-reduce.8.cloned.1.call-start = ((), (), s32[]{:S(2)}) async-start(), calls=%async_computation.5 | async-start | bytes 196608 | tf_op jit(solution)/shard_map/psum | solution.py:118
  161.3 11.8 %collective-permute-start.12 = (f32[256,384]{0,1:T(8,128)S(1)}, f32[256,384]{0,1:T(8,128)S(1)}, u32[]{:S(2)}, u32[]{:S(2)}) collective-permute-start(f32[256,384]{0,1:T(8,128)S(1)} %get-tuple-element.45), channel_id=1, source_target_pairs={{1,0},{2,1},{3,2},{4,3},{5,4},{6,5},{7,6},{9,8},{10,9},{11,10},{12... | collective-permute-start | bytes 1179656 | tf_op jit(solution)/shard_map/ppermute | solution.py:25
  173.4 11.9 %collective-permute-start.11 = (f32[256,384]{0,1:T(8,128)S(1)}, f32[256,384]{0,1:T(8,128)S(1)}, u32[]{:S(2)}, u32[]{:S(2)}) collective-permute-start(f32[256,384]{0,1:T(8,128)S(1)} %get-tuple-element.64), channel_id=1, source_target_pairs={{0,1},{1,2},{2,3},{3,4},{4,5},{5,6},{6,7},{8,9},{9,10},{10,11},{11... | collective-permute-start | bytes 1179656 | tf_op jit(solution)/shard_map/ppermute | solution.py:25
  186.7 10.1 %collective-permute-start.14 = (f32[256,384]{0,1:T(8,128)S(1)}, f32[256,384]{0,1:T(8,128)S(1)}, u32[]{:S(2)}, u32[]{:S(2)}) collective-permute-start(f32[256,384]{0,1:T(8,128)S(1)} %get-tuple-element.39), channel_id=1, source_target_pairs={{1,0},{2,1},{3,2},{4,3},{5,4},{6,5},{7,6},{9,8},{10,9},{11,10},{12... | collective-permute-start | bytes 1179656 | tf_op jit(solution)/shard_map/ppermute | solution.py:25
  197.1 11.1 %collective-permute-start.13 = (f32[256,384]{0,1:T(8,128)S(1)}, f32[256,384]{0,1:T(8,128)S(1)}, u32[]{:S(2)}, u32[]{:S(2)}) collective-permute-start(f32[256,384]{0,1:T(8,128)S(1)} %get-tuple-element.62), channel_id=1, source_target_pairs={{0,1},{1,2},{2,3},{3,4},{4,5},{5,6},{6,7},{8,9},{9,10},{10,11},{11... | collective-permute-start | bytes 1179656 | tf_op jit(solution)/shard_map/ppermute | solution.py:25
  245.4 183.2 %all-reduce.10.cloned.1.call-start = ((), (), s32[]{:S(2)}) async-start(), calls=%async_computation.6 | async-start | bytes 196608 | tf_op jit(solution)/shard_map/psum | solution.py:118
  305.5 11.8 %collective-permute-start.23 = (f32[256,384]{0,1:T(8,128)S(1)}, f32[256,384]{0,1:T(8,128)S(1)}, u32[]{:S(2)}, u32[]{:S(2)}) collective-permute-start(f32[256,384]{0,1:T(8,128)S(1)} %get-tuple-element.35), channel_id=1, source_target_pairs={{1,0},{2,1},{3,2},{4,3},{5,4},{6,5},{7,6},{9,8},{10,9},{11,10},{12... | collective-permute-start | bytes 1179656 | tf_op jit(solution)/shard_map/ppermute | solution.py:25
  317.7 11.9 %collective-permute-start.22 = (f32[256,384]{0,1:T(8,128)S(1)}, f32[256,384]{0,1:T(8,128)S(1)}, u32[]{:S(2)}, u32[]{:S(2)}) collective-permute-start(f32[256,384]{0,1:T(8,128)S(1)} %get-tuple-element.60), channel_id=1, source_target_pairs={{0,1},{1,2},{2,3},{3,4},{4,5},{5,6},{6,7},{8,9},{9,10},{10,11},{11... | collective-permute-start | bytes 1179656 | tf_op jit(solution)/shard_map/ppermute | solution.py:25
  331.0 10.1 %collective-permute-start.25 = (f32[256,384]{0,1:T(8,128)S(1)}, f32[256,384]{0,1:T(8,128)S(1)}, u32[]{:S(2)}, u32[]{:S(2)}) collective-permute-start(f32[256,384]{0,1:T(8,128)S(1)} %get-tuple-element.29), channel_id=1, source_target_pairs={{1,0},{2,1},{3,2},{4,3},{5,4},{6,5},{7,6},{9,8},{10,9},{11,10},{12... | collective-permute-start | bytes 1179656 | tf_op jit(solution)/shard_map/ppermute | solution.py:25
  341.5 11.1 %collective-permute-start.24 = (f32[256,384]{0,1:T(8,128)S(1)}, f32[256,384]{0,1:T(8,128)S(1)}, u32[]{:S(2)}, u32[]{:S(2)}) collective-permute-start(f32[256,384]{0,1:T(8,128)S(1)} %get-tuple-element.58), channel_id=1, source_target_pairs={{0,1},{1,2},{2,3},{3,4},{4,5},{5,6},{6,7},{8,9},{9,10},{10,11},{11... | collective-permute-start | bytes 1179656 | tf_op jit(solution)/shard_map/ppermute | solution.py:25
  389.8 183.2 %all-reduce.12.cloned.1.call-start = ((), (), s32[]{:S(2)}) async-start(), calls=%async_computation.7 | async-start | bytes 196608 | tf_op jit(solution)/shard_map/psum | solution.py:118
  449.9 11.8 %collective-permute-start.34 = (f32[256,384]{0,1:T(8,128)S(1)}, f32[256,384]{0,1:T(8,128)S(1)}, u32[]{:S(2)}, u32[]{:S(2)}) collective-permute-start(f32[256,384]{0,1:T(8,128)S(1)} %get-tuple-element.25), channel_id=1, source_target_pairs={{1,0},{2,1},{3,2},{4,3},{5,4},{6,5},{7,6},{9,8},{10,9},{11,10},{12... | collective-permute-start | bytes 1179656 | tf_op jit(solution)/shard_map/ppermute | solution.py:25
  462.0 11.9 %collective-permute-start.33 = (f32[256,384]{0,1:T(8,128)S(1)}, f32[256,384]{0,1:T(8,128)S(1)}, u32[]{:S(2)}, u32[]{:S(2)}) collective-permute-start(f32[256,384]{0,1:T(8,128)S(1)} %get-tuple-element.56), channel_id=1, source_target_pairs={{0,1},{1,2},{2,3},{3,4},{4,5},{5,6},{6,7},{8,9},{9,10},{10,11},{11... | collective-permute-start | bytes 1179656 | tf_op jit(solution)/shard_map/ppermute | solution.py:25
  475.5 10.1 %collective-permute-start.36 = (f32[256,384]{0,1:T(8,128)S(1)}, f32[256,384]{0,1:T(8,128)S(1)}, u32[]{:S(2)}, u32[]{:S(2)}) collective-permute-start(f32[256,384]{0,1:T(8,128)S(1)} %get-tuple-element.19), channel_id=1, source_target_pairs={{1,0},{2,1},{3,2},{4,3},{5,4},{6,5},{7,6},{9,8},{10,9},{11,10},{12... | collective-permute-start | bytes 1179656 | tf_op jit(solution)/shard_map/ppermute | solution.py:25
  485.9 11.1 %collective-permute-start.35 = (f32[256,384]{0,1:T(8,128)S(1)}, f32[256,384]{0,1:T(8,128)S(1)}, u32[]{:S(2)}, u32[]{:S(2)}) collective-permute-start(f32[256,384]{0,1:T(8,128)S(1)} %get-tuple-element.54), channel_id=1, source_target_pairs={{0,1},{1,2},{2,3},{3,4},{4,5},{5,6},{6,7},{8,9},{9,10},{10,11},{11... | collective-permute-start | bytes 1179656 | tf_op jit(solution)/shard_map/ppermute | solution.py:25
  594.3 11.8 %collective-permute-start.45 = (f32[256,384]{0,1:T(8,128)S(1)}, f32[256,384]{0,1:T(8,128)S(1)}, u32[]{:S(2)}, u32[]{:S(2)}) collective-permute-start(f32[256,384]{0,1:T(8,128)S(1)} %get-tuple-element.15), channel_id=1, source_target_pairs={{1,0},{2,1},{3,2},{4,3},{5,4},{6,5},{7,6},{9,8},{10,9},{11,10},{12... | collective-permute-start | bytes 1179656 | tf_op jit(solution)/shard_map/ppermute | solution.py:25
  606.4 11.9 %collective-permute-start.44 = (f32[256,384]{0,1:T(8,128)S(1)}, f32[256,384]{0,1:T(8,128)S(1)}, u32[]{:S(2)}, u32[]{:S(2)}) collective-permute-start(f32[256,384]{0,1:T(8,128)S(1)} %get-tuple-element.52), channel_id=1, source_target_pairs={{0,1},{1,2},{2,3},{3,4},{4,5},{5,6},{6,7},{8,9},{9,10},{10,11},{11... | collective-permute-start | bytes 1179656 | tf_op jit(solution)/shard_map/ppermute | solution.py:25
  620.0 10.1 %collective-permute-start.47 = (f32[256,384]{0,1:T(8,128)S(1)}, f32[256,384]{0,1:T(8,128)S(1)}, u32[]{:S(2)}, u32[]{:S(2)}) collective-permute-start(f32[256,384]{0,1:T(8,128)S(1)} %get-tuple-element.9), channel_id=1, source_target_pairs={{1,0},{2,1},{3,2},{4,3},{5,4},{6,5},{7,6},{9,8},{10,9},{11,10},{12... | collective-permute-start | bytes 1179656 | tf_op jit(solution)/shard_map/ppermute | solution.py:25
  631.2 10.9 %collective-permute-start.46 = (f32[256,384]{0,1:T(8,128)}, f32[256,384]{0,1:T(8,128)}, u32[]{:S(2)}, u32[]{:S(2)}) collective-permute-start(f32[256,384]{0,1:T(8,128)} %get-tuple-element.50), channel_id=1, source_target_pairs={{0,1},{1,2},{2,3},{3,4},{4,5},{5,6},{6,7},{8,9},{9,10},{10,11},{11... | collective-permute-start | bytes 1179656 | tf_op jit(solution)/shard_map/ppermute | solution.py:25
  (79 other events, 608.7 us)
Sparse Core Ops, SparseCore 0:
  100.3 39.7 all-reduce.5
  245.6 38.6 all-reduce.7
  389.9 38.6 all-reduce.9
  534.4 38.5 all-reduce.11
